TPU v7x, 32 devices: a 4x4x1 block of a 4x4x8 slice. The times are simulated.
32 devices in a mesh: dp: 1 (over z), ep: 32 (over y, x, core).
Axes of the slice: x: 4, y: 4, z: 1, core: 2. Of those that a mesh axis runs over, the one named last changes fastest.
The devices are a block of a 4x4x8 slice.
Arguments:
- tokens: bfloat16 [16384, 2048], P(('dp', 'ep'))
- route_idx: int32 [16384, 6], P(('dp', 'ep'))
- gate_vals: float32 [16384, 6], P(('dp', 'ep'))
- w_gate: bfloat16 [64, 2048, 1408], P('ep')
- w_up: bfloat16 [64, 2048, 1408], P('ep')
- w_down: bfloat16 [64, 1408, 2048], P('ep')
Outputs:
- output: bfloat16 [16384, 2048], P(('dp', 'ep'))
All inputs are finite; a program needn't handle non-finite values.
Results may differ from a plain program's by a relative error of at most 0.00786291.
Values are sent between devices in bfloat16 or wider.
A program may use at most 768 MiB of HBM per device.

v0:
```python
import jax
import jax.numpy as jnp
from jax import lax
from jax.sharding import PartitionSpec as P


def pack_index(route_loc, n_experts, capacity):
    hit_mask = route_loc[:, :, None] == jnp.arange(n_experts)
    member = jnp.sum(hit_mask, axis=1, dtype=jnp.int32)
    running = jnp.cumsum(member, axis=0)
    targets = jnp.arange(capacity) + 1
    row_ids = jax.vmap(lambda column: jnp.searchsorted(column, targets, side="left"), in_axes=1)(running)
    slot_pos = jnp.take_along_axis(running, route_loc, axis=1) - 1
    return row_ids, slot_pos


def combine_rows(returned, flat_pos, gate_loc):
    picked = jnp.take(returned, flat_pos, axis=0)
    return jnp.sum(gate_loc[:, :, None] * picked.astype(jnp.float32), axis=1).astype(jnp.bfloat16)


def expert_ffn(rows_in, wg_loc, wu_loc, wd_loc):
    pre_gate = jnp.einsum("erd,edf->erf", rows_in, wg_loc, preferred_element_type=jnp.float32)
    pre_up = jnp.einsum("erd,edf->erf", rows_in, wu_loc, preferred_element_type=jnp.float32)
    hidden = (jax.nn.silu(pre_gate) * pre_up).astype(jnp.bfloat16)
    return jnp.einsum("erf,efd->erd", hidden, wd_loc, preferred_element_type=jnp.float32).astype(jnp.bfloat16)


def solution(mesh):
    group_n = mesh.shape["ep"]
    row_spec = P(("dp", "ep"))
    expert_spec = P("ep")

    def local_step(tok_loc, route_loc, gate_loc, wg_loc, wu_loc, wd_loc):
        local_n = wg_loc.shape[0]
        tok_dev, d_model = tok_loc.shape
        capacity = tok_dev // 2
        row_ids, slot_pos = pack_index(route_loc, local_n * group_n, capacity)
        row_ids = row_ids.reshape(group_n, local_n, capacity).transpose(1, 0, 2)
        send_buf = jnp.take(tok_loc, row_ids, axis=0, mode="fill", fill_value=0)
        recv_buf = lax.all_to_all(send_buf, "ep", 1, 1, tiled=True)
        expert_out = expert_ffn(recv_buf.reshape(local_n, group_n * capacity, d_model), wg_loc, wu_loc, wd_loc)
        returned = lax.all_to_all(expert_out.reshape(local_n, group_n, capacity, d_model), "ep", 1, 1, tiled=True)
        flat_pos = ((route_loc % local_n) * group_n + route_loc // local_n) * capacity + slot_pos
        return combine_rows(returned.reshape(-1, d_model), flat_pos, gate_loc)

    return jax.shard_map(local_step, mesh=mesh, in_specs=(row_spec, row_spec, row_spec, expert_spec, expert_spec, expert_spec), out_specs=row_spec, check_vma=False)
```

profile of v0, /device:TPU:97, one launch (start us, length us, event | category | flops | bytes accessed | tf_op | source)
XLA Modules:
  0.0 3731.5 jit_solution(7910548100785397011)
XLA Ops:
  0.0 0.0 copy-start
  0.0 1.0 convert_reduce_fusion
  1.0 1.2 reduce-window.6
  2.2 0.2 slice_reduce_fusion
  2.5 0.8 fusion.11
  3.2 1297.2 %while.24 = (s32[]{:T(128)}, u32[64,256]{1,0:T(8,128)S(1)}, u32[64,256]{1,0:T(8,128)S(1)}, s32[64,512]{1,0:T(8,128)S(1)}, s32[]{:T(128)}, /*index=5*/s32[]{:T(128)}) while((s32[]{:T(128)}, u32[64,256]{1,0:T(8,128)S(1)}, u32[64,256]{1,0:T(8,128)S(1)}, s32[64,512]{1,0:T(8,128)S(1)}, s32[]{:T(128)}, /*index=5*/s32[]{:T(128)}) %tuple.35), condition=%wide.region_4.5_spmd.clone, body=%wide.region_3.4_spmd.clone.sunk | while | flops 377091 | bytes 1345617 | solution.py:12
  3.3 129.5 %gather_fusion = s32[16384]{0:T(1024)S(1)} fusion(s32[64,512]{1,0:T(8,128)S(1)} %get-tuple-element.146, u32[16384]{0:T(1024)S(1)} %bitcast.49), kind=kCustom, calls=%fused_computation.clone.clone.1 | custom fusion | bytes 262144 | tf_op jit(solution)/shard_map/vmap(jit(searchsorted))/vmap(jit(_searchsorted_scan_impl))/while/body/eval_jaxpr/gather | solution.py:12
  132.9 0.1 select_select_fusion.5
  133.0 129.5 %gather_fusion = s32[16384]{0:T(1024)S(1)} fusion(s32[64,512]{1,0:T(8,128)S(1)} %get-tuple-element.146, u32[16384]{0:T(1024)S(1)} %bitcast.49), kind=kCustom, calls=%fused_computation.clone.clone.1 | custom fusion | bytes 262144 | tf_op jit(solution)/shard_map/vmap(jit(searchsorted))/vmap(jit(_searchsorted_scan_impl))/while/body/eval_jaxpr/gather | solution.py:12
  262.6 0.1 select_select_fusion.5
  262.7 129.5 %gather_fusion = s32[16384]{0:T(1024)S(1)} fusion(s32[64,512]{1,0:T(8,128)S(1)} %get-tuple-element.146, u32[16384]{0:T(1024)S(1)} %bitcast.49), kind=kCustom, calls=%fused_computation.clone.clone.1 | custom fusion | bytes 262144 | tf_op jit(solution)/shard_map/vmap(jit(searchsorted))/vmap(jit(_searchsorted_scan_impl))/while/body/eval_jaxpr/gather | solution.py:12
  392.3 0.1 select_select_fusion.5
  392.5 129.5 %gather_fusion = s32[16384]{0:T(1024)S(1)} fusion(s32[64,512]{1,0:T(8,128)S(1)} %get-tuple-element.146, u32[16384]{0:T(1024)S(1)} %bitcast.49), kind=kCustom, calls=%fused_computation.clone.clone.1 | custom fusion | bytes 262144 | tf_op jit(solution)/shard_map/vmap(jit(searchsorted))/vmap(jit(_searchsorted_scan_impl))/while/body/eval_jaxpr/gather | solution.py:12
  522.0 0.1 select_select_fusion.5
  522.2 129.5 %gather_fusion = s32[16384]{0:T(1024)S(1)} fusion(s32[64,512]{1,0:T(8,128)S(1)} %get-tuple-element.146, u32[16384]{0:T(1024)S(1)} %bitcast.49), kind=kCustom, calls=%fused_computation.clone.clone.1 | custom fusion | bytes 262144 | tf_op jit(solution)/shard_map/vmap(jit(searchsorted))/vmap(jit(_searchsorted_scan_impl))/while/body/eval_jaxpr/gather | solution.py:12
  651.7 0.1 select_select_fusion.5
  651.9 129.5 %gather_fusion = s32[16384]{0:T(1024)S(1)} fusion(s32[64,512]{1,0:T(8,128)S(1)} %get-tuple-element.146, u32[16384]{0:T(1024)S(1)} %bitcast.49), kind=kCustom, calls=%fused_computation.clone.clone.1 | custom fusion | bytes 262144 | tf_op jit(solution)/shard_map/vmap(jit(searchsorted))/vmap(jit(_searchsorted_scan_impl))/while/body/eval_jaxpr/gather | solution.py:12
  781.5 0.1 select_select_fusion.5
  781.6 129.5 %gather_fusion = s32[16384]{0:T(1024)S(1)} fusion(s32[64,512]{1,0:T(8,128)S(1)} %get-tuple-element.146, u32[16384]{0:T(1024)S(1)} %bitcast.49), kind=kCustom, calls=%fused_computation.clone.clone.1 | custom fusion | bytes 262144 | tf_op jit(solution)/shard_map/vmap(jit(searchsorted))/vmap(jit(_searchsorted_scan_impl))/while/body/eval_jaxpr/gather | solution.py:12
  911.2 0.1 select_select_fusion.5
  911.3 129.5 %gather_fusion = s32[16384]{0:T(1024)S(1)} fusion(s32[64,512]{1,0:T(8,128)S(1)} %get-tuple-element.146, u32[16384]{0:T(1024)S(1)} %bitcast.49), kind=kCustom, calls=%fused_computation.clone.clone.1 | custom fusion | bytes 262144 | tf_op jit(solution)/shard_map/vmap(jit(searchsorted))/vmap(jit(_searchsorted_scan_impl))/while/body/eval_jaxpr/gather | solution.py:12
  1040.9 0.1 select_select_fusion.5
  1041.1 129.5 %gather_fusion = s32[16384]{0:T(1024)S(1)} fusion(s32[64,512]{1,0:T(8,128)S(1)} %get-tuple-element.146, u32[16384]{0:T(1024)S(1)} %bitcast.49), kind=kCustom, calls=%fused_computation.clone.clone.1 | custom fusion | bytes 262144 | tf_op jit(solution)/shard_map/vmap(jit(searchsorted))/vmap(jit(_searchsorted_scan_impl))/while/body/eval_jaxpr/gather | solution.py:12
  1170.6 0.1 select_select_fusion.5
  1170.8 129.5 %gather_fusion = s32[16384]{0:T(1024)S(1)} fusion(s32[64,512]{1,0:T(8,128)S(1)} %get-tuple-element.146, u32[16384]{0:T(1024)S(1)} %bitcast.49), kind=kCustom, calls=%fused_computation.clone.clone.1 | custom fusion | bytes 262144 | tf_op jit(solution)/shard_map/vmap(jit(searchsorted))/vmap(jit(_searchsorted_scan_impl))/while/body/eval_jaxpr/gather | solution.py:12
  1300.3 0.1 select_select_fusion.5
  1300.6 0.6 copy.63
  1301.2 0.0 copy-done
  1301.2 0.0 copy-start.4
  1301.2 80.3 %gather_fusion.1 = bf16[16384,2048]{1,0:T(8,128)(2,1)} fusion(bf16[512,2048]{1,0:T(8,128)(2,1)S(1)} %copy-done, s32[16384]{0:T(1024)S(1)} %broadcast_clamp_fusion), kind=kCustom, calls=%fused_computation.1 | custom fusion | bytes 134283264 | tf_op jit(solution)/shard_map/jit(_take)/gather | solution.py:40
  1381.5 0.0 copy-done.4
  1381.5 44.5 %copy_select_fusion = bf16[2,32,256,2048]{3,2,0,1:T(8,128)(2,1)} fusion(bf16[2,32,256,2048]{3,2,1,0:T(8,128)(2,1)} %bitcast.4, pred[2,32,256]{2,0,1:T(4,128)(4,1)S(1)} %copy-done.4), kind=kLoop, calls=%fused_computation.13 | loop fusion | flops 33554432 | bytes 134234112 | tf_op jit(solution)/shard_map/jit(_take)/select_n | solution.py:40
  1426.1 875.6 %all_to_all.10 = bf16[2,32,256,2048]{3,2,0,1:T(8,128)(2,1)} all-to-all(bf16[2,32,256,2048]{3,2,0,1:T(8,128)(2,1)} %copy_select_fusion), channel_id=1, replica_groups=mesh['dp'=1,'ep'=32] {'ep'}, dimensions={1} | all-to-all | bytes 134217728 | tf_op jit(solution)/shard_map/all_to_all | solution.py:41
  2301.6 44.1 %copy.65 = bf16[2,32,256,2048]{3,2,1,0:T(8,128)(2,1)} copy(bf16[2,32,256,2048]{3,2,0,1:T(8,128)(2,1)} %all_to_all.10) | data formatting | bytes 134217728 | tf_op jit(solution)/shard_map/all_to_all | solution.py:41
  2345.7 115.3 %fusion.12 = f32[2,8192,1408]{2,1,0:T(8,128)} fusion(bf16[2,8192,2048]{2,1,0:T(8,128)(2,1)} %bitcast.5, bf16[2,2048,1408]{2,1,0:T(8,128)(2,1)} %param.11), kind=kOutput, calls=%fused_computation.45 | convolution fusion | flops 94489280512 | bytes 170917888 | tf_op jit(solution)/shard_map/erd,edf->erf/dot_general | solution.py:23
  2461.0 119.2 %multiply_convert_fusion = bf16[2,8192,1408]{2,1,0:T(8,128)(2,1)} fusion(f32[2,8192,1408]{2,1,0:T(8,128)} %fusion.12, bf16[2,8192,2048]{2,1,0:T(8,128)(2,1)} %bitcast.5, bf16[2,2048,1408]{2,1,0:T(8,128)(2,1)} %param.12), kind=kOutput, calls=%fused_computation.12 | convolution fusion | flops 94627692544 | bytes 217055232 | tf_op jit(solution)/shard_map/erd,edf->erf/dot_general | solution.py:24
  2580.2 113.8 %convolution_convert_fusion = bf16[2,8192,2048]{2,1,0:T(8,128)(2,1)} fusion(bf16[2,8192,1408]{2,1,0:T(8,128)(2,1)} %multiply_convert_fusion, bf16[2,1408,2048]{2,1,0:T(8,128)(2,1)} %param.13), kind=kOutput, calls=%fused_computation.14 | convolution fusion | flops 94522834944 | bytes 124780544 | tf_op jit(solution)/shard_map/erf,efd->erd/dot_general | solution.py:26
  2694.0 44.0 %copy.66 = bf16[2,32,256,2048]{3,2,0,1:T(8,128)(2,1)} copy(bf16[2,32,256,2048]{3,2,1,0:T(8,128)(2,1)} %bitcast.6) | data formatting | bytes 134217728 | tf_op jit(solution)/shard_map/reshape | solution.py:43
  2738.0 0.0 copy-start.3
  2738.0 7.6 all-to-all-start.1
  2745.6 0.0 copy-done.3
  2745.6 0.0 copy-start.2
  2745.7 0.1 copy.59
  2745.8 0.2 reshape.74
  2746.0 0.6 copy-done.2
  2746.5 0.0 copy-start.5
  2746.5 24.9 gather_fusion.3
  2771.5 0.2 reshape.77
  2771.7 0.1 copy.60
  2771.8 0.1 copy.68
  2772.0 0.2 reshape.68
  2772.2 0.2 copy.61
  2772.3 0.0 copy-done.5
  2772.4 0.1 copy.56
  2772.5 801.6 %all-to-all-done.1 = bf16[2,32,256,2048]{3,2,0,1:T(8,128)(2,1)} async-done(((bf16[2,32,256,2048]{3,2,0,1:T(8,128)(2,1)}), bf16[2,32,256,2048]{3,2,0,1:T(8,128)(2,1)}, u32[]{:S(2)}, u32[]{:S(2)}) %all-to-all-start.1) | async-done | bytes 67108896 | tf_op jit(solution)/shard_map/all_to_all | solution.py:43
  3574.1 44.0 %copy.67 = bf16[2,32,256,2048]{3,2,1,0:T(8,128)(2,1)} copy(bf16[2,32,256,2048]{3,2,0,1:T(8,128)(2,1)} %all-to-all-done.1) | data formatting | bytes 134217728 | tf_op jit(solution)/shard_map/all_to_all | solution.py:43
  3618.2 72.1 %gather_fusion.2 = bf16[3072,2048]{1,0:T(8,128)(2,1)} fusion(bf16[16384,2048]{1,0:T(8,128)(2,1)} %bitcast.7, s32[3072]{0:T(1024)S(1)} %broadcast_clamp_fusion.1), kind=kCustom, calls=%fused_computation.2 | custom fusion | bytes 25178112 | tf_op jit(solution)/shard_map/jit(_take)/gather | solution.py:18
  3690.2 0.0 copy-start.1
  3690.2 20.5 reshape.67
  3710.7 20.6 multiply_reduce_fusion
  3731.3 0.0 copy-done.1
  (74 shorter events, 1.4 us)
Async XLA Ops:
  0.0 1301.2 %copy-start = (bf16[512,2048]{1,0:T(8,128)(2,1)S(1)}, bf16[512,2048]{1,0:T(8,128)(2,1)}, u32[]{:S(2)}) copy-start(bf16[512,2048]{1,0:T(8,128)(2,1)} %param.8) | copy-start | bytes 6291460
  1301.2 80.3 %copy-start.4 = (pred[2,32,256]{2,0,1:T(4,128)(4,1)S(1)}, pred[2,32,256]{2,0,1:T(4,128)(4,1)}, u32[]{:S(2)}) copy-start(pred[2,32,256]{2,0,1:T(4,128)(4,1)} %copy.63) | copy-start | bytes 49156
  2738.0 7.6 copy-start.3
  2738.0 836.1 %all-to-all-start.1 = ((bf16[2,32,256,2048]{3,2,0,1:T(8,128)(2,1)}), bf16[2,32,256,2048]{3,2,0,1:T(8,128)(2,1)}, u32[]{:S(2)}, u32[]{:S(2)}) async-start(bf16[2,32,256,2048]{3,2,0,1:T(8,128)(2,1)} %copy.66), calls=%async_computation.1 | async-start | bytes 134217728 | tf_op jit(solution)/shard_map/all_to_all | solution.py:43
  2745.6 0.9 copy-start.2
  2746.5 25.8 copy-start.5
  3690.2 41.1 %copy-start.1 = (bf16[512,2048]{1,0:T(8,128)(2,1)S(1)}, bf16[512,2048]{1,0:T(8,128)(2,1)}, u32[]{:S(2)}) copy-start(bf16[512,2048]{1,0:T(8,128)(2,1)} %param.8) | copy-start | bytes 6291460
where the time goes:
time: 3800 us; the launch traced here: 3730 us
  local copies, waits for them, and re-layouts  1630 us (43%)
  blocking collectives  876 us (23%)
  waiting for transfers between devices  802 us (21%)
  matrix products  348 us (9%)
  other arithmetic  69.3 us (2%)
    gather x10, local copies, waits for them, and re-layouts, pack_index(): jnp.searchsorted(column, targets, side='left')  1290 us
    all_to_all x1, blocking collectives, local_step(): recv_buf = lax.all_to_all(send_buf, 'ep', 1, 1, tiled=True)  876 us
    all_to_all x1, waiting for transfers between devices, local_step(): lax.all_to_all(expert_out.reshape(local_n, group_n, capacity, d_model), '...  802 us
    dot_general x1, matrix products, expert_ffn(): jnp.einsum('erd,edf->erf', rows_in, wu_loc, preferred_element_type=jnp.fl...  119 us
    dot_general x1, matrix products, expert_ffn(): jnp.einsum('erd,edf->erf', rows_in, wg_loc, preferred_element_type=jnp.fl...  115 us
    dot_general x1, matrix products, expert_ffn(): jnp.einsum('erf,efd->erd', hidden, wd_loc, preferred_element_type=jnp.flo...  114 us
    gather x2, local copies, waits for them, and re-layouts, combine_rows(): picked = jnp.take(returned, flat_pos, axis=0)  92.6 us
    gather x1, local copies, waits for them, and re-layouts, local_step(): send_buf = jnp.take(tok_loc, row_ids, axis=0, mode='fill', fill_value=0)  80.3 us
  transfers between devices with their start and end apart: 1, of which 1 were waited for; matrix products, arithmetic and copies ran while one was open for 1% of the time, Pallas kernels for 0%

commit v1 on v0

v1 whole, which is shorter than its diff:
```python
import functools

import jax
import jax.numpy as jnp
from jax import lax
from jax.experimental import pallas as pl
from jax.experimental.pallas import tpu as pltpu
from jax.sharding import PartitionSpec as P

CHUNKS = 4
GROUP = 512
TILE = 256
SMALL = 64


def expert_kernel(counts, x_ref, pos_ref, gate_ref, wg_ref, wu_ref, wd_ref, out_ref):
    step = pl.program_id(0)
    local_n = wg_ref.shape[0]
    out_ref[...] = jnp.zeros_like(out_ref)

    def run_tile(expert, first, rows):
        ranks = pos_ref[0, expert : expert + 1, :] - first
        row_id = lax.broadcasted_iota(jnp.int32, (rows, ranks.shape[1]), 0)
        pick = jnp.where(row_id == ranks, 1.0, 0.0).astype(jnp.bfloat16)
        picked = jnp.dot(pick, x_ref[...], preferred_element_type=jnp.float32).astype(jnp.bfloat16)
        pre_gate = jnp.dot(picked, wg_ref[expert], preferred_element_type=jnp.float32)
        pre_up = jnp.dot(picked, wu_ref[expert], preferred_element_type=jnp.float32)
        hidden = (jax.nn.silu(pre_gate) * pre_up).astype(jnp.bfloat16)
        rows_out = jnp.dot(hidden, wd_ref[expert], preferred_element_type=jnp.float32).astype(jnp.bfloat16)
        placed = lax.dot_general(pick, rows_out, (((0,), (0,)), ((), ())), preferred_element_type=jnp.float32)
        out_ref[...] += gate_ref[:, expert : expert + 1] * placed

    for expert in range(local_n):
        count = counts[step, expert]

        @pl.when((count > 0) & (count <= SMALL))
        def _():
            run_tile(expert, 0, SMALL)

        @pl.when(count > SMALL)
        def _():
            def body(tile, carry):
                run_tile(expert, tile * TILE, TILE)
                return carry

            lax.fori_loop(0, (count + TILE - 1) // TILE, body, 0)


def run_experts(x_rows, ranks, gates, counts, wg_loc, wu_loc, wd_loc):
    n_rows, d_model = x_rows.shape
    local_n, _, d_ff = wg_loc.shape
    groups = n_rows // GROUP
    whole = functools.partial(pl.BlockSpec, pipeline_mode=pl.Buffered(1))
    return pl.pallas_call(
        expert_kernel,
        out_shape=jax.ShapeDtypeStruct((n_rows, d_model), jnp.float32),
        grid_spec=pltpu.PrefetchScalarGridSpec(
            num_scalar_prefetch=1,
            grid=(groups,),
            in_specs=[
                pl.BlockSpec((GROUP, d_model), lambda g, c: (g, 0)),
                pl.BlockSpec((1, local_n, GROUP), lambda g, c: (g, 0, 0)),
                pl.BlockSpec((GROUP, local_n), lambda g, c: (g, 0)),
                whole((local_n, d_model, d_ff), lambda g, c: (0, 0, 0)),
                whole((local_n, d_model, d_ff), lambda g, c: (0, 0, 0)),
                whole((local_n, d_ff, d_model), lambda g, c: (0, 0, 0)),
            ],
            out_specs=pl.BlockSpec((GROUP, d_model), lambda g, c: (g, 0)),
        ),
        compiler_params=pltpu.CompilerParams(vmem_limit_bytes=60 * 1024 * 1024),
        cost_estimate=pl.CostEstimate(
            flops=groups * TILE * 6 * d_model * d_ff,
            bytes_accessed=n_rows * d_model * 6,
            transcendentals=0,
        ),
    )(counts, x_rows, ranks, gates, wg_loc, wu_loc, wd_loc)


def solution(mesh):
    group_n = mesh.shape["ep"]
    row_spec = P(("dp", "ep"))
    expert_spec = P("ep")

    def local_step(tok_loc, route_loc, gate_loc, wg_loc, wu_loc, wd_loc):
        local_n = wg_loc.shape[0]
        tok_dev, d_model = tok_loc.shape
        n_experts = local_n * group_n
        chunk = tok_dev // CHUNKS
        groups = group_n * chunk // GROUP
        gathered = [
            lax.all_gather(tok_loc[c * chunk : (c + 1) * chunk], "ep", tiled=True) for c in range(CHUNKS)
        ]
        hit = route_loc[None, :, :] == jnp.arange(n_experts)[:, None, None]
        pair_gate = jnp.sum(jnp.where(hit, gate_loc[None], 0.0), axis=2)
        mine = lax.all_to_all(pair_gate.reshape(group_n, local_n, tok_dev), "ep", 0, 0, tiled=True)
        mine = mine.reshape(group_n, local_n, CHUNKS, chunk).transpose(2, 1, 0, 3)
        mine = mine.reshape(CHUNKS, local_n, groups, GROUP).transpose(0, 2, 1, 3)
        member = (mine > 0).astype(jnp.bfloat16)
        before = jnp.triu(jnp.ones((GROUP, GROUP), jnp.bfloat16))
        running = jnp.dot(member, before, preferred_element_type=jnp.float32).astype(jnp.int32)
        ranks = jnp.where(mine > 0, running - 1, -GROUP)
        counts = running[..., -1]
        gates = mine.transpose(0, 1, 3, 2).reshape(CHUNKS, groups * GROUP, local_n)

        outs = []
        for c in range(CHUNKS):
            partial = run_experts(gathered[c], ranks[c], gates[c], counts[c], wg_loc, wu_loc, wd_loc)
            outs.append(lax.psum_scatter(partial, "ep", scatter_dimension=0, tiled=True))
        return jnp.concatenate(outs, axis=0).astype(jnp.bfloat16)

    return jax.shard_map(
        local_step,
        mesh=mesh,
        in_specs=(row_spec, row_spec, row_spec, expert_spec, expert_spec, expert_spec),
        out_specs=row_spec,
        check_vma=False,
    )
```

time: 3800 us -> 940 us (0.25); the launches traced: 3730 us -> 937 us
  local copies, waits for them, and re-layouts: 1630 us -> 15.6 us
  blocking collectives: 876 us -> 0 us
  matrix products: 348 us -> 0.28 us
  Pallas kernels: 0 us -> 328 us
  waiting for transfers between devices: 802 us -> 563 us
  other arithmetic: 69.3 us -> 6.99 us
    gather x18 -> x0, local copies, waits for them, and re-layouts: 1490 us -> none  [the longest x10 1290 us: pack_index(): jnp.searchsorted(column, targets, side='left')]
    all_to_all x1 -> x0, blocking collectives: 876 us -> none  [local_step(): recv_buf = lax.all_to_all(send_buf, 'ep', 1, 1, tiled=True)]
    all_to_all x1, waiting for transfers between devices: 802 us -> 8.57 us  [local_step(): lax.all_to_all(pair_gate.reshape(group_n, local_n, tok_dev), 'ep', 0, 0,...]
    reduce_scatter x0 -> x4, waiting for transfers between devices: none -> 504 us  [local_step(): lax.psum_scatter(partial, 'ep', scatter_dimension=0, tiled=True)]
    dot_general x3 -> x1, matrix products: 348 us -> 0.28 us  [local_step(): jnp.dot(member, before, preferred_element_type=jnp.float32)]
    pallas_call x0 -> x4, Pallas kernels: none -> 328 us  [run_experts(): pl.pallas_call(expert_kernel, out_shape=jax.ShapeDtypeStruct((n_rows, d_m...]
    all_to_all x2 -> x0, local copies, waits for them, and re-layouts: 88.1 us -> none  [the longest x1 44.1 us: local_step(): recv_buf = lax.all_to_all(send_buf, 'ep', 1, 1, tiled=True)]
    all_gather x0 -> x4, waiting for transfers between devices: none -> 47.6 us  [local_step(): lax.all_gather(tok_loc[c * chunk:(c + 1) * chunk], 'ep', tiled=True)]
  transfers between devices with their start and end apart: 1 -> 9, of which waited for: 1 -> 6; matrix products, arithmetic and copies ran while one was open for 1% -> 2% of each run, Pallas kernels for 0% -> 35%
where the time goes in v1:
time: 940 us; the launch traced here: 937 us
  waiting for transfers between devices  563 us (60%)
  Pallas kernels  328 us (35%)
  local copies, waits for them, and re-layouts  15.6 us (2%)
  between operations  14 us (1%)
  starting transfers between devices  9.59 us (1%)
    reduce_scatter x4, waiting for transfers between devices, local_step(): lax.psum_scatter(partial, 'ep', scatter_dimension=0, tiled=True)  504 us
    pallas_call x4, Pallas kernels, run_experts(): pl.pallas_call(expert_kernel, out_shape=jax.ShapeDtypeStruct((n_rows, d_m...  328 us
    all_gather x4, waiting for transfers between devices, local_step(): lax.all_gather(tok_loc[c * chunk:(c + 1) * chunk], 'ep', tiled=True)  47.6 us
  transfers between devices with their start and end apart: 9, of which 6 were waited for; matrix products, arithmetic and copies ran while one was open for 2% of the time, Pallas kernels for 35%

profile of v1, /device:TPU:97, one launch (start us, length us, event | category | flops | bytes accessed | tf_op | source)
XLA Modules:
  0.0 937.3 jit_solution(1830474997524455057)
XLA Ops:
  6.5 0.0 copy-start.1
  6.5 0.0 copy-start
  6.6 0.0 all-gather.5.cloned.1.call-start
  6.6 2.9 fusion.9
  9.5 0.1 all-gather.5.cloned.1.call-update
  9.5 0.1 all-gather.7.cloned.1.call-start
  9.6 0.7 all-gather.7.cloned.1.call-update
  10.4 0.1 all-gather.9.cloned.1.call-start
  10.4 0.7 all-gather.9.cloned.1.call-update
  11.2 0.1 all-gather.11.cloned.1.call-start
  11.2 0.6 all-gather.11.cloned.1.call-update
  11.8 0.0 copy-done.1
  11.8 0.0 copy-done
  11.8 0.1 select_reduce_fusion
  11.9 0.7 reshape.28
  12.6 9.1 all-to-all-start
  21.8 0.1 reduce-scatter.5.cloned.1.call-start
  21.9 8.6 all-to-all-done
  30.4 0.1 reshape.32
  30.6 0.1 copy.125
  30.7 0.3 fusion.2
  31.0 0.1 copy_convert_fusion
  31.1 0.1 fusion.11
  31.2 0.1 copy.97
  31.3 0.7 copy.98.counts
  32.0 2.0 copy.112
  34.0 0.2 add_select_fusion
  34.1 0.7 slice_bitcast_fusion.3
  34.8 47.6 %all-gather.5.cloned.1.call-done.x_ref = bf16[4096,2048]{1,0:T(8,128)(2,1)} async-done(((bf16[128,2048]{1,0:T(8,128)(2,1)}), bf16[4096,2048]{1,0:T(8,128)(2,1)}) %all-gather.5.cloned.1.call-update) | async-done | bytes 16777232 | tf_op jit(solution)/shard_map/all_gather | solution.py:91
  82.4 81.9 %shard_map.64 = f32[4096,2048]{1,0:T(8,128)} custom-call(s32[8,2]{1,0:T(8,128)} %copy.98.counts, bf16[4096,2048]{1,0:T(8,128)(2,1)} %all-gather.5.cloned.1.call-done.x_ref, s32[8,2,512]{2,1,0:T(2,128)} %get-tuple-element.13.pos_ref, f32[4096,2]{1,0:T(8,128)} %bitcast.31, bf16[2,2048,1408]{2,1,0:T(8,128)(2,1)} %wg_ref.7, bf16[2,2048,1408]{2,1,0:T(8,128)(2,1)} %wu_ref.7, ...), custom_call_target="tpu_custom_call" | custom-call | flops 35433480192 | bytes 50331648 | tf_op jit(solution)/shard_map/pallas_call | solution.py:54
  164.3 0.1 reduce-scatter.5.cloned.1.call-update
  164.4 0.1 reduce-scatter.7.cloned.1.call-start
  164.5 0.1 copy.100
  164.6 0.7 copy.101.counts
  165.2 2.0 copy.113
  167.2 0.0 all-gather.7.cloned.1.call-done.x_ref
  167.2 82.2 %shard_map.65 = f32[4096,2048]{1,0:T(8,128)} custom-call(s32[8,2]{1,0:T(8,128)} %copy.101.counts, bf16[4096,2048]{1,0:T(8,128)(2,1)} %all-gather.7.cloned.1.call-done.x_ref, s32[8,2,512]{2,1,0:T(2,128)} %get-tuple-element.16.pos_ref, f32[4096,2]{1,0:T(8,128)} %bitcast.33, bf16[2,2048,1408]{2,1,0:T(8,128)(2,1)} %wg_ref.7, bf16[2,2048,1408]{2,1,0:T(8,128)(2,1)} %wu_ref.7, ...), custom_call_target="tpu_custom_call" | custom-call | flops 35433480192 | bytes 50331648 | tf_op jit(solution)/shard_map/pallas_call | solution.py:54
  249.4 0.1 reduce-scatter.7.cloned.1.call-update
  249.5 0.1 reduce-scatter.9.cloned.1.call-start
  249.5 0.1 copy.103
  249.6 0.7 copy.104.counts
  250.3 2.0 copy.114
  252.3 0.0 all-gather.9.cloned.1.call-done.x_ref
  252.3 81.9 %shard_map.66 = f32[4096,2048]{1,0:T(8,128)} custom-call(s32[8,2]{1,0:T(8,128)} %copy.104.counts, bf16[4096,2048]{1,0:T(8,128)(2,1)} %all-gather.9.cloned.1.call-done.x_ref, s32[8,2,512]{2,1,0:T(2,128)} %get-tuple-element.15.pos_ref, f32[4096,2]{1,0:T(8,128)} %bitcast.34, bf16[2,2048,1408]{2,1,0:T(8,128)(2,1)} %wg_ref.7, bf16[2,2048,1408]{2,1,0:T(8,128)(2,1)} %wu_ref.7, ...), custom_call_target="tpu_custom_call" | custom-call | flops 35433480192 | bytes 50331648 | tf_op jit(solution)/shard_map/pallas_call | solution.py:54
  334.2 0.1 reduce-scatter.9.cloned.1.call-update
  334.3 0.1 reduce-scatter.11.cloned.1.call-start
  334.3 0.1 copy.106
  334.4 0.7 copy.108.counts
  335.1 2.0 copy.107
  337.1 0.0 all-gather.11.cloned.1.call-done.x_ref
  337.1 81.9 %shard_map.67 = f32[4096,2048]{1,0:T(8,128)} custom-call(s32[8,2]{1,0:T(8,128)} %copy.108.counts, bf16[4096,2048]{1,0:T(8,128)(2,1)} %all-gather.11.cloned.1.call-done.x_ref, s32[8,2,512]{2,1,0:T(2,128)} %get-tuple-element.14.pos_ref, f32[4096,2]{1,0:T(8,128)} %bitcast.32, bf16[2,2048,1408]{2,1,0:T(8,128)(2,1)} %wg_ref.7, bf16[2,2048,1408]{2,1,0:T(8,128)(2,1)} %wu_ref.7, ...), custom_call_target="tpu_custom_call" | custom-call | flops 35433480192 | bytes 50331648 | tf_op jit(solution)/shard_map/pallas_call | solution.py:54
  419.0 0.1 reduce-scatter.11.cloned.1.call-update
  419.0 28.4 %reduce-scatter.5.cloned.1.call-done = f32[128,2048]{1,0:T(8,128)} async-done(((f32[4096,2048]{1,0:T(8,128)}), f32[128,2048]{1,0:T(8,128)}) %reduce-scatter.5.cloned.1.call-update) | async-done | bytes 1048592 | tf_op jit(solution)/shard_map/reduce_scatter | solution.py:108
  447.4 1.3 convert.12
  448.7 158.6 %reduce-scatter.7.cloned.1.call-done = f32[128,2048]{1,0:T(8,128)} async-done(((f32[4096,2048]{1,0:T(8,128)}), f32[128,2048]{1,0:T(8,128)}) %reduce-scatter.7.cloned.1.call-update) | async-done | bytes 1048592 | tf_op jit(solution)/shard_map/reduce_scatter | solution.py:108
  607.3 1.3 convert.13
  608.6 158.7 %reduce-scatter.9.cloned.1.call-done = f32[128,2048]{1,0:T(8,128)} async-done(((f32[4096,2048]{1,0:T(8,128)}), f32[128,2048]{1,0:T(8,128)}) %reduce-scatter.9.cloned.1.call-update) | async-done | bytes 1048592 | tf_op jit(solution)/shard_map/reduce_scatter | solution.py:108
  767.3 1.3 convert.14
  768.6 158.7 %reduce-scatter.11.cloned.1.call-done = f32[128,2048]{1,0:T(8,128)} async-done(((f32[4096,2048]{1,0:T(8,128)}), f32[128,2048]{1,0:T(8,128)}) %reduce-scatter.11.cloned.1.call-update) | async-done | bytes 1048592 | tf_op jit(solution)/shard_map/reduce_scatter | solution.py:108
  927.3 1.3 convert.15
  928.6 1.5 pad_maximum_fusion
  (5 shorter events, 0.1 us)
Async XLA Ops:
  6.5 5.2 copy-start.1
  6.5 5.3 copy-start
  6.6 75.8 %all-gather.5.cloned.1.call-start = ((), (), s32[]{:S(2)}) async-start(), calls=%async_computation.5 | async-start | bytes 17301504 | tf_op jit(solution)/shard_map/all_gather | solution.py:91
  9.5 157.7 %all-gather.7.cloned.1.call-start = ((), (), s32[]{:S(2)}) async-start(), calls=%async_computation.7 | async-start | bytes 17301504 | tf_op jit(solution)/shard_map/all_gather | solution.py:91
  10.4 241.9 %all-gather.9.cloned.1.call-start = ((), (), s32[]{:S(2)}) async-start(), calls=%async_computation.9 | async-start | bytes 17301504 | tf_op jit(solution)/shard_map/all_gather | solution.py:91
  11.2 325.9 %all-gather.11.cloned.1.call-start = ((), (), s32[]{:S(2)}) async-start(), calls=%async_computation.11 | async-start | bytes 17301504 | tf_op jit(solution)/shard_map/all_gather | solution.py:91
  12.6 17.8 %all-to-all-start = ((f32[32,2,512]{2,1,0:T(2,128)}), f32[32,2,512]{2,1,0:T(2,128)S(1)}, u32[]{:S(2)}, u32[]{:S(2)}) async-start(f32[32,2,512]{2,1,0:T(2,128)} %reshape.28), calls=%async_computation | async-start | bytes 262144 | tf_op jit(solution)/shard_map/all_to_all | solution.py:95
  21.8 425.7 %reduce-scatter.5.cloned.1.call-start = ((), (), s32[]{:S(2)}) async-start(), calls=%async_computation.6 | async-start | bytes 34603008 | tf_op jit(solution)/shard_map/reduce_scatter | solution.py:108
  164.4 442.9 %reduce-scatter.7.cloned.1.call-start = ((), (), s32[]{:S(2)}) async-start(), calls=%async_computation.8 | async-start | bytes 34603008 | tf_op jit(solution)/shard_map/reduce_scatter | solution.py:108
  249.5 517.8 %reduce-scatter.9.cloned.1.call-start = ((), (), s32[]{:S(2)}) async-start(), calls=%async_computation.10 | async-start | bytes 34603008 | tf_op jit(solution)/shard_map/reduce_scatter | solution.py:108
  334.3 593.1 %reduce-scatter.11.cloned.1.call-start = ((), (), s32[]{:S(2)}) async-start(), calls=%async_computation.12 | async-start | bytes 34603008 | tf_op jit(solution)/shard_map/reduce_scatter | solution.py:108
Sparse Core Ops, SparseCore 0:
  9.7 72.6 all-gather.4
  84.5 66.6 all-gather.6
  153.3 66.6 all-gather.8
  221.9 66.6 all-gather.10
  292.3 155.1 reduce-scatter.4
  451.0 156.2 reduce-scatter.6
  611.0 156.2 reduce-scatter.8
  771.0 156.2 reduce-scatter.10

commit v2 on v1

v2 whole, which is shorter than its diff:
```python
import functools

import jax
import jax.numpy as jnp
from jax import lax
from jax.experimental import pallas as pl
from jax.experimental.pallas import tpu as pltpu
from jax.sharding import PartitionSpec as P

CHUNKS = 4
GROUP = 1024
SMALL = 128
TILE = 256
COLS = 512


def expert_kernel(
    counts, x_ref, row_rank, col_rank, col_gate,
    wg_own, wu_own, wd_own, wg_peer, wu_peer, wd_peer,
    out_ref, wg_buf, wu_buf, wd_buf, acc, picked, w_sem, out_sem,
):
    group, expert = pl.program_id(0), pl.program_id(1)
    n_groups, n_experts = pl.num_programs(0), pl.num_programs(1)
    own_n = wg_own.shape[0]
    step = group * n_experts + expert
    slot = step % 2
    bufs = (wg_buf, wu_buf, wd_buf)

    def fetch(at, refs, index):
        for part, (ref, buf) in enumerate(zip(refs, bufs)):
            pltpu.make_async_copy(ref.at[index], buf.at[at % 2], w_sem.at[at % 2, part]).start()

    def fetch_step(at):
        index = at % n_experts

        @pl.when(index < own_n)
        def _():
            fetch(at, (wg_own, wu_own, wd_own), index)

        @pl.when(index >= own_n)
        def _():
            fetch(at, (wg_peer, wu_peer, wd_peer), index - own_n)

    def out_copy(at):
        rows = pl.ds(pl.multiple_of(at * GROUP, GROUP), GROUP)
        return pltpu.make_async_copy(acc, out_ref.at[rows], out_sem)

    @pl.when(step == 0)
    def _():
        fetch_step(step)

    @pl.when(step + 1 < n_groups * n_experts)
    def _():
        fetch_step(step + 1)

    @pl.when((expert == 0) & (group > 0))
    def _():
        out_copy(group - 1).wait()

    @pl.when(expert == 0)
    def _():
        acc[...] = jnp.zeros_like(acc)

    for part, (ref, buf) in enumerate(zip((wg_own, wu_own, wd_own), bufs)):
        pltpu.make_async_copy(ref.at[0], buf.at[slot], w_sem.at[slot, part]).wait()

    count = counts[group, expert]
    d_model = x_ref.shape[1]

    def run_tile(first, rows):
        row_id = lax.broadcasted_iota(jnp.int32, (rows, GROUP), 0)
        pick = jnp.where(row_id == row_rank[0, 0] - first, 1.0, 0.0).astype(jnp.bfloat16)
        for col in range(0, d_model, COLS):
            cols = slice(col, col + COLS)
            picked[:rows, cols] = jnp.dot(
                pick, x_ref[:, cols], preferred_element_type=jnp.float32
            ).astype(jnp.bfloat16)
        pre_gate = jnp.dot(picked[:rows, :], wg_buf[slot], preferred_element_type=jnp.float32)
        pre_up = jnp.dot(picked[:rows, :], wu_buf[slot], preferred_element_type=jnp.float32)
        hidden = (jax.nn.silu(pre_gate) * pre_up).astype(jnp.bfloat16)
        col_id = lax.broadcasted_iota(jnp.int32, (GROUP, rows), 1)
        put = jnp.where(col_id == col_rank[0] - first, 1.0, 0.0).astype(jnp.bfloat16)
        gate = col_gate[0]
        for col in range(0, d_model, COLS):
            cols = slice(col, col + COLS)
            rows_out = jnp.dot(hidden, wd_buf[slot, :, cols], preferred_element_type=jnp.float32)
            placed = jnp.dot(put, rows_out.astype(jnp.bfloat16), preferred_element_type=jnp.float32)
            acc[:, cols] += gate * placed

    @pl.when((count > 0) & (count <= SMALL))
    def _():
        run_tile(0, SMALL)

    @pl.when(count > SMALL)
    def _():
        def body(tile, carry):
            run_tile(tile * TILE, TILE)
            return carry

        lax.fori_loop(0, (count + TILE - 1) // TILE, body, 0)

    @pl.when(expert == n_experts - 1)
    def _():
        out_copy(group).start()

    @pl.when((expert == n_experts - 1) & (group == n_groups - 1))
    def _():
        out_copy(group).wait()


def run_experts(x_rows, ranks, gates, counts, own, peer):
    n_rows, d_model = x_rows.shape
    n_groups, n_experts = counts.shape
    d_ff = own[0].shape[2]
    hbm = pl.BlockSpec(memory_space=pl.ANY)
    column = pl.BlockSpec((1, GROUP, 1), lambda g, e, c: (e, g, 0))
    return pl.pallas_call(
        expert_kernel,
        out_shape=jax.ShapeDtypeStruct((n_rows, d_model), jnp.float32),
        grid_spec=pltpu.PrefetchScalarGridSpec(
            num_scalar_prefetch=1,
            grid=(n_groups, n_experts),
            in_specs=[
                pl.BlockSpec((GROUP, d_model), lambda g, e, c: (g, 0), pipeline_mode=pl.Buffered(1)),
                pl.BlockSpec((1, 1, 1, GROUP), lambda g, e, c: (e, g, 0, 0)),
                column,
                column,
            ]
            + [hbm] * 6,
            out_specs=hbm,
            scratch_shapes=[
                pltpu.VMEM((2, d_model, d_ff), jnp.bfloat16),
                pltpu.VMEM((2, d_model, d_ff), jnp.bfloat16),
                pltpu.VMEM((2, d_ff, d_model), jnp.bfloat16),
                pltpu.VMEM((GROUP, d_model), jnp.float32),
                pltpu.VMEM((TILE, d_model), jnp.bfloat16),
                pltpu.SemaphoreType.DMA((2, 3)),
                pltpu.SemaphoreType.DMA,
            ],
        ),
        compiler_params=pltpu.CompilerParams(vmem_limit_bytes=62 * 1024 * 1024),
        cost_estimate=pl.CostEstimate(
            flops=n_rows * 6 * d_model * d_ff, bytes_accessed=n_rows * d_model * 6, transcendentals=0
        ),
    )(
        counts,
        x_rows,
        ranks.reshape(n_experts, n_groups, 1, GROUP),
        ranks.reshape(n_experts, n_rows, 1),
        gates.reshape(n_experts, n_rows, 1),
        *own,
        *peer,
    )


def solution(mesh):
    group_n = mesh.shape["ep"]
    row_spec = P(("dp", "ep"))
    expert_spec = P("ep")
    pairs = [(j, j ^ 1) for j in range(group_n)]
    sides = [list(range(side, group_n, 2)) for side in range(2)]
    homes = group_n // 2

    def local_step(tok_loc, route_loc, gate_loc, wg_loc, wu_loc, wd_loc):
        own = (wg_loc, wu_loc, wd_loc)
        peer = tuple(lax.ppermute(w, "ep", pairs) for w in own)
        own_n = wg_loc.shape[0]
        shared_n = 2 * own_n
        tok_dev, d_model = tok_loc.shape
        n_experts = own_n * group_n
        chunk = tok_dev // CHUNKS
        n_groups = homes * chunk // GROUP
        gathered = [
            lax.all_gather(tok_loc[c * chunk : (c + 1) * chunk], "ep", tiled=True, axis_index_groups=sides)
            for c in range(CHUNKS)
        ]
        hit = route_loc[None, :, :] == jnp.arange(n_experts)[:, None, None]
        pair_gate = jnp.sum(jnp.where(hit, gate_loc[None], 0.0), axis=2)
        mine = lax.all_to_all(
            pair_gate.reshape(homes, shared_n, tok_dev), "ep", 0, 0, axis_index_groups=sides, tiled=True
        )
        mine = mine.reshape(homes, shared_n, CHUNKS, chunk).transpose(2, 1, 0, 3)
        mine = mine.reshape(CHUNKS, shared_n, n_groups, GROUP)
        mine = jnp.where(lax.axis_index("ep") % 2 == 0, mine, jnp.roll(mine, own_n, axis=1))
        member = (mine > 0).astype(jnp.bfloat16)
        before = jnp.triu(jnp.ones((GROUP, GROUP), jnp.bfloat16))
        running = jnp.dot(member, before, preferred_element_type=jnp.float32).astype(jnp.int32)
        ranks = jnp.where(mine > 0, running - 1, -GROUP)
        counts = running[..., -1].transpose(0, 2, 1)

        outs = []
        for c in range(CHUNKS):
            partial = run_experts(gathered[c], ranks[c], mine[c], counts[c], own, peer)
            outs.append(
                lax.psum_scatter(partial, "ep", scatter_dimension=0, tiled=True, axis_index_groups=sides)
            )
        return jnp.concatenate(outs, axis=0).astype(jnp.bfloat16)

    return jax.shard_map(
        local_step,
        mesh=mesh,
        in_specs=(row_spec, row_spec, row_spec, expert_spec, expert_spec, expert_spec),
        out_specs=row_spec,
        check_vma=False,
    )
```

time: 940 us -> 729 us (0.78)
  waiting for transfers between devices: 563 us -> 309 us
  local copies, waits for them, and re-layouts: 15.6 us -> 48.9 us
    reduce_scatter x4, waiting for transfers between devices: 504 us -> 264 us  [local_step(): lax.psum_scatter(partial, 'ep', scatter_dimension=0, tiled=True, axis_ind...]
    another operation x0 -> x8, local copies, waits for them, and re-layouts: none -> 43 us  [the longest x4 21.9 us: run_experts(): ranks.reshape(n_experts, n_rows, 1)]
    all_gather x4, waiting for transfers between devices: 47.6 us -> 16 us  [local_step(): lax.all_gather(tok_loc[c * chunk:(c + 1) * chunk], 'ep', tiled=True, axis...]
    ppermute x0 -> x3, waiting for transfers between devices: none -> 18.8 us  [local_step(): peer = tuple((lax.ppermute(w, 'ep', pairs) for w in own))]
  transfers between devices with their start and end apart: 9 -> 12, of which waited for: 6 -> 7; matrix products, arithmetic and copies ran while one was open for 2% -> 7% of each run, Pallas kernels for 35% -> 46%
where the time goes in v2:
time: 729 us; the launch traced here: 723 us
  Pallas kernels  333 us (46%)
  waiting for transfers between devices  309 us (42%)
  local copies, waits for them, and re-layouts  48.9 us (7%)
  between operations  13.9 us (2%)
  starting transfers between devices  11.2 us (2%)
    pallas_call x4, Pallas kernels, run_experts(): pl.pallas_call(expert_kernel, out_shape=jax.ShapeDtypeStruct((n_rows, d_m...  333 us
    reduce_scatter x4, waiting for transfers between devices, local_step(): lax.psum_scatter(partial, 'ep', scatter_dimension=0, tiled=True, axis_ind...  264 us
    another operation x4, local copies, waits for them, and re-layouts, run_experts(): ranks.reshape(n_experts, n_rows, 1)  21.9 us
    another operation x4, local copies, waits for them, and re-layouts, run_experts(): gates.reshape(n_experts, n_rows, 1)  21 us
    ppermute x3, waiting for transfers between devices, local_step(): peer = tuple((lax.ppermute(w, 'ep', pairs) for w in own))  18.8 us
    all_gather x4, waiting for transfers between devices, local_step(): lax.all_gather(tok_loc[c * chunk:(c + 1) * chunk], 'ep', tiled=True, axis...  16 us
  transfers between devices with their start and end apart: 12, of which 7 were waited for; matrix products, arithmetic and copies ran while one was open for 7% of the time, Pallas kernels for 46%

profile of v2, /device:TPU:97, one launch (start us, length us, event | category | flops | bytes accessed | tf_op | source)
XLA Modules:
  0.0 723.4 jit_solution(4043275615858262943)
XLA Ops:
  6.5 0.0 copy-start.1
  6.5 0.0 copy-start
  6.6 0.0 all-gather.5.cloned.1.call-start
  6.6 2.9 fusion.11
  9.4 0.1 all-gather.5.cloned.1.call-update
  9.5 0.1 all-gather.7.cloned.1.call-start
  9.6 0.7 all-gather.7.cloned.1.call-update
  10.3 0.1 all-gather.9.cloned.1.call-start
  10.4 0.7 all-gather.9.cloned.1.call-update
  11.1 0.1 all-gather.11.cloned.1.call-start
  11.2 0.6 all-gather.11.cloned.1.call-update
  11.8 2.1 collective-permute-start
  13.9 0.1 collective-permute-start.1
  14.0 0.4 collective-permute-start.2
  14.4 0.0 copy-done.1
  14.4 0.0 copy-done
  14.4 0.1 select_reduce_fusion
  14.5 0.7 reshape.11
  15.2 8.1 %all-to-all-start = ((f32[16,4,512]{2,1,0:T(4,128)}), f32[16,4,512]{2,1,0:T(4,128)S(1)}, u32[]{:S(2)}, u32[]{:S(2)}) async-start(f32[16,4,512]{2,1,0:T(4,128)} %reshape.11), calls=%async_computation | async-start | bytes 262144 | tf_op jit(solution)/shard_map/all_to_all | solution.py:179
  23.3 0.1 reduce-scatter.5.cloned.1.call-start
  23.4 8.1 %all-to-all-done = f32[16,4,512]{2,1,0:T(4,128)S(1)} async-done(((f32[16,4,512]{2,1,0:T(4,128)}), f32[16,4,512]{2,1,0:T(4,128)S(1)}, u32[]{:S(2)}, u32[]{:S(2)}) %all-to-all-start) | async-done | bytes 131104 | tf_op jit(solution)/shard_map/all_to_all | solution.py:179
  31.5 0.1 reshape.15
  31.6 0.1 reshape.13
  31.8 0.1 broadcast_compare_fusion
  32.0 0.7 add_select_fusion
  32.7 0.9 slice_reduce_fusion.7
  33.6 5.3 reshape_squeeze.48.col_rank
  38.8 0.1 slice.80
  38.9 0.1 copy.76
  39.0 0.4 slice_reduce_fusion.3
  39.4 5.3 reshape_squeeze.49.col_gate
  44.7 0.6 fusion.13
  45.3 0.0 collective-permute-done.wg_peer
  45.3 2.3 collective-permute-done.1.wu_peer
  47.7 16.5 %collective-permute-done.2.wd_peer = bf16[2,1408,2048]{2,1,0:T(8,128)(2,1)} collective-permute-done((bf16[2,1408,2048]{2,1,0:T(8,128)(2,1)}, bf16[2,1408,2048]{2,1,0:T(8,128)(2,1)}, u32[]{:S(2)}, u32[]{:S(2)}) %collective-permute-start.2) | collective-permute-done | bytes 11534368 | tf_op jit(solution)/shard_map/ppermute | solution.py:166
  64.2 16.0 %all-gather.5.cloned.1.call-done.x_ref = bf16[2048,2048]{1,0:T(8,128)(2,1)} async-done(((bf16[128,2048]{1,0:T(8,128)(2,1)}), bf16[2048,2048]{1,0:T(8,128)(2,1)}) %all-gather.5.cloned.1.call-update) | async-done | bytes 8388624 | tf_op jit(solution)/shard_map/all_gather | solution.py:174
  80.1 83.4 %shard_map.64 = f32[2048,2048]{1,0:T(8,128)} custom-call(s32[2,4]{1,0:T(2,128)} %bitcast.34, bf16[2048,2048]{1,0:T(8,128)(2,1)} %all-gather.5.cloned.1.call-done.x_ref, s32[4,2,1,1024]{3,2,1,0:T(1,128)} %get-tuple-element.19.row_rank, s32[4,2048,1]{2,1,0:T(8,128)} %reshape_squeeze.48.col_rank, f32[4,2048,1]{2,1,0:T(8,128)} %reshape_squeeze.49.col_gate, ...), custom_call_target="tpu_custom_call" | custom-call | flops 35433480192 | bytes 25165824 | tf_op jit(solution)/shard_map/pallas_call | solution.py:117
  163.6 0.1 reduce-scatter.5.cloned.1.call-update
  163.6 0.1 reduce-scatter.7.cloned.1.call-start
  163.7 5.7 reshape_squeeze.50.col_rank
  169.4 5.2 reshape_squeeze.51.col_gate
  174.7 0.0 all-gather.7.cloned.1.call-done.x_ref
  174.7 83.2 %shard_map.65 = f32[2048,2048]{1,0:T(8,128)} custom-call(s32[2,4]{1,0:T(2,128)} %bitcast.33, bf16[2048,2048]{1,0:T(8,128)(2,1)} %all-gather.7.cloned.1.call-done.x_ref, s32[4,2,1,1024]{3,2,1,0:T(1,128)} %get-tuple-element.20.row_rank, s32[4,2048,1]{2,1,0:T(8,128)} %reshape_squeeze.50.col_rank, f32[4,2048,1]{2,1,0:T(8,128)} %reshape_squeeze.51.col_gate, ...), custom_call_target="tpu_custom_call" | custom-call | flops 35433480192 | bytes 25165824 | tf_op jit(solution)/shard_map/pallas_call | solution.py:117
  257.9 0.1 reduce-scatter.7.cloned.1.call-update
  258.0 0.1 reduce-scatter.9.cloned.1.call-start
  258.1 5.4 reshape_squeeze.52.col_rank
  263.5 5.2 reshape_squeeze.53.col_gate
  268.7 0.0 all-gather.9.cloned.1.call-done.x_ref
  268.7 83.2 %shard_map.66 = f32[2048,2048]{1,0:T(8,128)} custom-call(s32[2,4]{1,0:T(2,128)} %bitcast.32, bf16[2048,2048]{1,0:T(8,128)(2,1)} %all-gather.9.cloned.1.call-done.x_ref, s32[4,2,1,1024]{3,2,1,0:T(1,128)} %get-tuple-element.21.row_rank, s32[4,2048,1]{2,1,0:T(8,128)} %reshape_squeeze.52.col_rank, f32[4,2048,1]{2,1,0:T(8,128)} %reshape_squeeze.53.col_gate, ...), custom_call_target="tpu_custom_call" | custom-call | flops 35433480192 | bytes 25165824 | tf_op jit(solution)/shard_map/pallas_call | solution.py:117
  351.9 0.1 reduce-scatter.9.cloned.1.call-update
  352.0 0.1 reduce-scatter.11.cloned.1.call-start
  352.1 5.5 reshape_squeeze.54.col_rank
  357.6 5.3 reshape_squeeze.55.col_gate
  362.9 83.2 %shard_map.67 = f32[2048,2048]{1,0:T(8,128)} custom-call(s32[2,4]{1,0:T(2,128)} %bitcast.31, bf16[2048,2048]{1,0:T(8,128)(2,1)} %all-gather.11.cloned.1.call-done.x_ref, s32[4,2,1,1024]{3,2,1,0:T(1,128)} %get-tuple-element.22.row_rank, s32[4,2048,1]{2,1,0:T(8,128)} %reshape_squeeze.54.col_rank, f32[4,2048,1]{2,1,0:T(8,128)} %reshape_squeeze.55.col_gate, ...), custom_call_target="tpu_custom_call" | custom-call | flops 35433480192 | bytes 25165824 | tf_op jit(solution)/shard_map/pallas_call | solution.py:117
  446.1 0.1 reduce-scatter.11.cloned.1.call-update
  446.2 0.0 reduce-scatter.5.cloned.1.call-done
  446.2 1.3 convert.12
  447.5 49.7 %reduce-scatter.7.cloned.1.call-done = f32[128,2048]{1,0:T(8,128)} async-done(((f32[2048,2048]{1,0:T(8,128)}), f32[128,2048]{1,0:T(8,128)}) %reduce-scatter.7.cloned.1.call-update) | async-done | bytes 1048592 | tf_op jit(solution)/shard_map/reduce_scatter | solution.py:195
  497.2 1.3 convert.13
  498.5 106.9 %reduce-scatter.9.cloned.1.call-done = f32[128,2048]{1,0:T(8,128)} async-done(((f32[2048,2048]{1,0:T(8,128)}), f32[128,2048]{1,0:T(8,128)}) %reduce-scatter.9.cloned.1.call-update) | async-done | bytes 1048592 | tf_op jit(solution)/shard_map/reduce_scatter | solution.py:195
  605.4 1.3 convert.14
  606.7 106.9 %reduce-scatter.11.cloned.1.call-done = f32[128,2048]{1,0:T(8,128)} async-done(((f32[2048,2048]{1,0:T(8,128)}), f32[128,2048]{1,0:T(8,128)}) %reduce-scatter.11.cloned.1.call-update) | async-done | bytes 1048592 | tf_op jit(solution)/shard_map/reduce_scatter | solution.py:195
  713.6 1.3 convert.15
  714.9 1.5 pad_maximum_fusion
  (6 shorter events, 0.2 us)
Async XLA Ops:
  6.5 7.8 %copy-start.1 = (s32[512,6]{0,1:T(8,128)S(1)}, s32[512,6]{0,1:T(8,128)}, u32[]{:S(2)}) copy-start(s32[512,6]{0,1:T(8,128)} %param.7) | copy-start | bytes 36868
  6.5 7.8 %copy-start = (f32[512,6]{0,1:T(8,128)S(1)}, f32[512,6]{0,1:T(8,128)}, u32[]{:S(2)}) copy-start(f32[512,6]{0,1:T(8,128)} %param.8) | copy-start | bytes 36868
  6.6 73.6 %all-gather.5.cloned.1.call-start = ((), (), s32[]{:S(2)}) async-start(), calls=%async_computation.5 | async-start | bytes 8912896 | tf_op jit(solution)/shard_map/all_gather | solution.py:174
  9.5 165.2 %all-gather.7.cloned.1.call-start = ((), (), s32[]{:S(2)}) async-start(), calls=%async_computation.7 | async-start | bytes 8912896 | tf_op jit(solution)/shard_map/all_gather | solution.py:174
  10.3 258.4 %all-gather.9.cloned.1.call-start = ((), (), s32[]{:S(2)}) async-start(), calls=%async_computation.9 | async-start | bytes 8912896 | tf_op jit(solution)/shard_map/all_gather | solution.py:174
  11.1 351.7 %all-gather.11.cloned.1.call-start = ((), (), s32[]{:S(2)}) async-start(), calls=%async_computation.11 | async-start | bytes 8912896 | tf_op jit(solution)/shard_map/all_gather | solution.py:174
  11.8 33.6 %collective-permute-start = (bf16[2,2048,1408]{2,1,0:T(8,128)(2,1)}, bf16[2,2048,1408]{2,1,0:T(8,128)(2,1)}, u32[]{:S(2)}, u32[]{:S(2)}) collective-permute-start(bf16[2,2048,1408]{2,1,0:T(8,128)(2,1)} %wg_own.7), channel_id=1, source_target_pairs={{0,1},{1,0},{2,3},{3,2},{4,5},{5,4},{6,7},{7,6},{8,9},{9,8},{10,11... | collective-permute-start | bytes 34603016 | tf_op jit(solution)/shard_map/ppermute | solution.py:166
  13.9 33.8 %collective-permute-start.1 = (bf16[2,2048,1408]{2,1,0:T(8,128)(2,1)}, bf16[2,2048,1408]{2,1,0:T(8,128)(2,1)}, u32[]{:S(2)}, u32[]{:S(2)}) collective-permute-start(bf16[2,2048,1408]{2,1,0:T(8,128)(2,1)} %wu_own.7), channel_id=1, source_target_pairs={{0,1},{1,0},{2,3},{3,2},{4,5},{5,4},{6,7},{7,6},{8,9},{9,8},{10,11... | collective-permute-start | bytes 34603016 | tf_op jit(solution)/shard_map/ppermute | solution.py:166
  14.0 50.1 %collective-permute-start.2 = (bf16[2,1408,2048]{2,1,0:T(8,128)(2,1)}, bf16[2,1408,2048]{2,1,0:T(8,128)(2,1)}, u32[]{:S(2)}, u32[]{:S(2)}) collective-permute-start(bf16[2,1408,2048]{2,1,0:T(8,128)(2,1)} %wd_own.7), channel_id=1, source_target_pairs={{0,1},{1,0},{2,3},{3,2},{4,5},{5,4},{6,7},{7,6},{8,9},{9,8},{10,11... | collective-permute-start | bytes 34603016 | tf_op jit(solution)/shard_map/ppermute | solution.py:166
  15.2 16.3 %all-to-all-start = ((f32[16,4,512]{2,1,0:T(4,128)}), f32[16,4,512]{2,1,0:T(4,128)S(1)}, u32[]{:S(2)}, u32[]{:S(2)}) async-start(f32[16,4,512]{2,1,0:T(4,128)} %reshape.11), calls=%async_computation | async-start | bytes 262144 | tf_op jit(solution)/shard_map/all_to_all | solution.py:179
  23.3 422.9 %reduce-scatter.5.cloned.1.call-start = ((), (), s32[]{:S(2)}) async-start(), calls=%async_computation.6 | async-start | bytes 17825792 | tf_op jit(solution)/shard_map/reduce_scatter | solution.py:195
  163.6 333.6 %reduce-scatter.7.cloned.1.call-start = ((), (), s32[]{:S(2)}) async-start(), calls=%async_computation.8 | async-start | bytes 17825792 | tf_op jit(solution)/shard_map/reduce_scatter | solution.py:195
  258.0 347.4 %reduce-scatter.9.cloned.1.call-start = ((), (), s32[]{:S(2)}) async-start(), calls=%async_computation.10 | async-start | bytes 17825792 | tf_op jit(solution)/shard_map/reduce_scatter | solution.py:195
  352.0 361.6 %reduce-scatter.11.cloned.1.call-start = ((), (), s32[]{:S(2)}) async-start(), calls=%async_computation.12 | async-start | bytes 17825792 | tf_op jit(solution)/shard_map/reduce_scatter | solution.py:195
Sparse Core Ops, SparseCore 0:
  9.6 70.4 all-gather.4
  82.1 65.2 all-gather.6
  149.3 65.0 all-gather.8
  216.3 65.1 all-gather.10
  284.6 104.5 reduce-scatter.4
  392.3 104.8 reduce-scatter.6
  500.4 104.8 reduce-scatter.8
  608.6 104.9 reduce-scatter.10
